TPU v7x, 512 devices: a whole 4x4x16 slice. The times are simulated.
512 devices in a mesh: frames: 32 (over y, x, core), heads: 16 (over z).
Axes of the slice: x: 4, y: 4, z: 16, core: 2. Of those that a mesh axis runs over, the one named last changes fastest.
Arguments:
- frames: bfloat16 [32768, 1152], P('frames', 'heads'), may hold values from -6 to 6
- latents: bfloat16 [256, 1152], P('frames'), may hold values from -400 to 400
- w_query: bfloat16 [1152, 4096], P(None, 'heads'), may hold values from -0.1875 to 0.1875
- w_key: bfloat16 [1152, 4096], P(None, 'heads'), may hold values from -0.1875 to 0.1875
- w_value: bfloat16 [1152, 4096], P(None, 'heads'), may hold values from -0.1875 to 0.1875
- w_out: bfloat16 [4096, 8192], P('heads', 'frames'), may hold values from -0.09375 to 0.09375
- norm_gain: float32 [8192], P('frames'), may hold values from 0.5 to 1.5
- w_gate: bfloat16 [8192, 16384], P('frames', 'heads'), may hold values from -0.0625 to 0.0625
- w_up: bfloat16 [8192, 16384], P('frames', 'heads'), may hold values from -0.0625 to 0.0625
- w_down: bfloat16 [16384, 8192], P('heads', 'frames'), may hold values from -0.046875 to 0.046875
Outputs:
- block_out: bfloat16 [256, 8192], P('heads', 'frames')
All inputs are finite; a program needn't handle non-finite values.
Results may differ from a plain program's by a relative error of at most 0.023.
Values may be sent and summed in bfloat16 or wider, within the bound.
No kernel may reach another device: no remote copies, remote signals or barrier semaphores. Data moves between devices by JAX's collectives and lax.ppermute only.
A program may use at most 64 MiB of HBM per device.

v0:
```python
import jax
import jax.numpy as jnp
from jax import lax
from jax.sharding import Mesh
from jax.sharding import PartitionSpec as P

HDIM = 128
D = 8192
FRAMES = ("frames_0", "frames_1", "frames_2")
BF16 = jnp.bfloat16
F32 = jnp.float32
norm_eps = 1e-06


def exchange(blocks, axis):
    return lax.all_to_all(blocks, axis, split_axis=0, concat_axis=0, tiled=True)


def collect_rows(array, axis):
    peers = lax.axis_size(axis)
    blocks = exchange(jnp.broadcast_to(array[None], (peers, *array.shape)), axis)
    return blocks.reshape(peers * array.shape[0], *array.shape[1:])


def sum_rows_at_owner(array, axis):
    peers = lax.axis_size(axis)
    blocks = array.astype(BF16).reshape(peers, array.shape[0] // peers, *array.shape[1:])
    return jnp.sum(exchange(blocks, axis).astype(F32), axis=0)


def split_terms(array, count):
    terms = []
    for _ in range(count):
        term = lax.reduce_precision(array, 8, 7)
        terms.append(term.astype(BF16))
        array = array - term
    return terms


def joined_terms(terms):
    array = terms[-1].astype(F32)
    for term in terms[-2::-1]:
        array = array + term.astype(F32)
    return array


def merged_softmax(local_max, total, mixed):
    peers = lax.axis_size(FRAMES)
    rows, heads = local_max.shape
    share = rows // peers
    terms = jnp.stack(split_terms(local_max, 3) + split_terms(total, 3), axis=-1)
    stats = terms.reshape(peers, share * heads * 6)
    stats = jnp.pad(stats, ((0, 0), (0, -stats.shape[1] % HDIM))).reshape(peers, -1, HDIM)
    body = mixed.astype(BF16).reshape(peers, share * heads, HDIM)
    arrived = exchange(jnp.concatenate([body, stats], axis=1), FRAMES)
    body = arrived[:, : share * heads].reshape(peers, share, heads, HDIM).astype(F32)
    stats = arrived[:, share * heads :].reshape(peers, -1)[:, : share * heads * 6]
    stats = stats.reshape(peers, share, heads, 6)
    part_max = joined_terms([stats[..., k] for k in range(3)])
    part_total = joined_terms([stats[..., k] for k in range(3, 6)])
    scale = jnp.exp(part_max - jnp.max(part_max, axis=0))
    total = jnp.sum(part_total * scale, axis=0)
    mixed = jnp.sum(body * scale[..., None], axis=0)
    return (mixed / total[..., None]).reshape(share, heads * HDIM).astype(BF16)


def on_device(frames, latents, w_query, w_key, w_value, w_out, norm_gain, w_gate, w_up, w_down):
    local_query = jnp.dot(latents, w_query, preferred_element_type=F32).astype(BF16)
    queries = collect_rows(local_query, FRAMES)
    width = w_key.shape[1]
    piece = lax.all_gather(frames, "heads", axis=1, tiled=True)
    keys = jnp.dot(piece, w_key, preferred_element_type=F32)
    values = jnp.dot(piece, w_value, preferred_element_type=F32)
    heads_here = width // HDIM
    latent_count = queries.shape[0]
    query_heads = queries.reshape(latent_count, heads_here, HDIM)
    key_heads = keys.astype(BF16).reshape(-1, heads_here, HDIM)
    value_heads = values.astype(BF16).reshape(-1, heads_here, HDIM)
    scores = jnp.einsum(
        "qhd,khd->qhk", query_heads, key_heads, preferred_element_type=F32
    ) * HDIM ** (-0.5)
    local_max = jnp.max(scores, axis=2)
    weights = jnp.exp(scores - local_max[:, :, None])
    total = jnp.sum(weights, axis=2)
    mixed = jnp.einsum(
        "qhk,khd->qhd", weights.astype(BF16), value_heads, preferred_element_type=F32
    )
    attention = collect_rows(merged_softmax(local_max, total, mixed), FRAMES)
    latent_state = sum_rows_at_owner(
        jnp.dot(attention, w_out, preferred_element_type=F32), "heads"
    ).astype(BF16)
    latent_full = collect_rows(latent_state, "heads")
    full_float = latent_full.astype(F32)
    square_part = jnp.sum(full_float * full_float, axis=1)
    normed = (full_float * norm_gain[None, :]).astype(BF16)
    gate_part = jnp.dot(normed, w_gate, preferred_element_type=F32).astype(BF16)
    up_part = jnp.dot(normed, w_up, preferred_element_type=F32).astype(BF16)
    square_terms = jnp.stack(split_terms(square_part, 2), axis=1)
    square_terms = jnp.pad(square_terms, ((0, 0), (0, 126)))
    peers = lax.axis_size(FRAMES)
    packed = jnp.concatenate([gate_part, up_part, square_terms], axis=1)
    sums = jnp.sum(exchange(packed.reshape(peers, -1, packed.shape[1]), FRAMES).astype(F32), axis=0)
    units = w_gate.shape[1]
    gate_sum, up_sum = (sums[:, :units], sums[:, units : 2 * units])
    squares = sums[:, 2 * units : 2 * units + 1] + sums[:, 2 * units + 1 : 2 * units + 2]
    scale_rows = lax.rsqrt(squares / D + norm_eps)
    hidden = (jax.nn.silu(gate_sum * scale_rows) * (up_sum * scale_rows)).astype(BF16)
    hidden_full = collect_rows(hidden, FRAMES)
    down = sum_rows_at_owner(jnp.dot(hidden_full, w_down, preferred_element_type=F32), "heads")
    return (latent_state.astype(F32) + down).astype(BF16)


def solution(mesh):
    torus = Mesh(
        mesh.devices.reshape(4, 4, 2, mesh.shape["heads"]),
        ("frames_0", "frames_1", "frames_2", "heads"),
    )
    placed = (
        P(FRAMES, "heads"),
        P(FRAMES, None),
        P(None, "heads"),
        P(None, "heads"),
        P(None, "heads"),
        P("heads", FRAMES),
        P(FRAMES),
        P(FRAMES, "heads"),
        P(FRAMES, "heads"),
        P("heads", FRAMES),
    )
    return jax.shard_map(
        on_device, mesh=torus, in_specs=placed, out_specs=P("heads", FRAMES), check_vma=False
    )
```

profile of v0, /device:TPU:32, one launch (start us, length us, event | category | flops | bytes accessed | tf_op | source)
XLA Modules:
  0.0 226.5 jit_solution(6184290056534508303)
XLA Ops:
  6.5 0.7 all-gather.2.cloned.1.call-update
  7.3 1.3 convolution_convert_fusion.7
  8.6 14.9 %all_to_all.40 = bf16[32,8,256]{2,1,0:T(8,128)(2,1)S(1)} all-to-all(bf16[32,8,256]{2,1,0:T(8,128)(2,1)S(1)} %broadcast_in_dim.8), channel_id=1, replica_groups=mesh['frames_0'=4,'frames_1'=4,'frames_2'=2,'heads'=16] {'frames_0','fra..., dimensions={0} | all-to-all | bytes 262144 | tf_op jit(solution)/shard_map/all_to_all | solution.py:16
  23.5 63.2 %all-gather.2.cloned.1.call-done = bf16[1024,1152]{0,1:T(8,128)(2,1)} async-done(((bf16[1024,72]{0,1:T(8,128)(2,1)}), bf16[1024,1152]{0,1:T(8,128)(2,1)}) %all-gather.2.cloned.1.call-update) | async-done | bytes 2359312 | tf_op jit(solution)/shard_map/all_gather | solution.py:71
  86.7 2.5 %convolution_convert_fusion.2 = bf16[1024,256]{0,1:T(8,128)(2,1)S(1)} fusion(bf16[1024,1152]{0,1:T(8,128)(2,1)} %all-gather.2.cloned.1.call-done, bf16[1152,256]{1,0:T(8,128)(2,1)S(1)} %copy-done), kind=kOutput, calls=%fused_computation.10 | convolution fusion | flops 604241920 | bytes 3473408 | tf_op jit(solution)/shard_map/dot_general | solution.py:72
  89.3 0.0 copy-start.7
  89.3 0.5 bitcast_reduce_fusion
  89.8 0.4 fusion.2
  90.2 0.8 copy-done.6
  90.9 0.1 copy-done.7
  91.0 0.9 convolution_convert_fusion.3
  91.9 0.0 copy-start.4
  92.0 0.5 fusion.4
  92.5 0.0 copy-start.5
  92.5 0.0 copy-start.1
  92.5 0.1 copy.82
  92.7 0.2 copy.83
  92.9 0.2 reshape.184
  93.1 0.0 copy-start.2
  93.1 15.2 %all_to_all.41 = bf16[32,17,128]{2,1,0:T(8,128)(2,1)S(1)} all-to-all(bf16[32,17,128]{2,1,0:T(8,128)(2,1)S(1)} %pad_maximum_fusion), channel_id=1, replica_groups=mesh['frames_0'=4,'frames_1'=4,'frames_2'=2,'heads'=16] {'frames_0','fra..., dimensions={0} | all-to-all | bytes 278528 | tf_op jit(solution)/shard_map/all_to_all | solution.py:16
  108.3 0.1 copy.85
  108.5 0.1 fusion.32
  108.6 0.1 subtract_exponential_fusion
  108.7 0.2 fusion.20
  108.9 0.1 copy.91
  109.0 0.1 copy.86
  109.0 0.1 multiply_reduce_fusion.1
  109.2 0.1 fusion.19
  109.3 11.4 %all_to_all.42 = bf16[32,8,256]{2,1,0:T(8,128)(2,1)S(1)} all-to-all(bf16[32,8,256]{2,1,0:T(8,128)(2,1)S(1)} %broadcast_in_dim.9), channel_id=1, replica_groups=mesh['frames_0'=4,'frames_1'=4,'frames_2'=2,'heads'=16] {'frames_0','fra..., dimensions={0} | all-to-all | bytes 262144 | tf_op jit(solution)/shard_map/all_to_all | solution.py:16
  120.7 0.2 convolution_convert_fusion.5
  120.9 22.1 %all_to_all.43 = bf16[16,16,256]{2,1,0:T(8,128)(2,1)S(1)} all-to-all(bf16[16,16,256]{2,1,0:T(8,128)(2,1)S(1)} %bitcast.85), channel_id=1, replica_groups=mesh['frames_0'=4,'frames_1'=4,'frames_2'=2,'heads'=16] {'heads'}, dimensions={0} | all-to-all | bytes 262144 | tf_op jit(solution)/shard_map/all_to_all | solution.py:16
  143.1 19.1 %all_to_all.44 = bf16[16,16,256]{2,1,0:T(8,128)(2,1)S(1)} all-to-all(bf16[16,16,256]{2,1,0:T(8,128)(2,1)S(1)} %broadcast_in_dim.10), channel_id=1, replica_groups=mesh['frames_0'=4,'frames_1'=4,'frames_2'=2,'heads'=16] {'heads'}, dimensions={0} | all-to-all | bytes 262144 | tf_op jit(solution)/shard_map/all_to_all | solution.py:16
  162.2 0.1 multiply_reduce_fusion
  162.4 0.1 reduce_sum.79
  162.5 0.1 copy.92
  162.7 0.3 convolution_convert_fusion
  163.0 0.3 convolution_convert_fusion.1
  163.3 0.1 fusion.6
  163.4 0.0 copy-start.3
  163.4 22.0 %all_to_all.45 = bf16[32,8,2176]{2,1,0:T(8,128)(2,1)S(1)} all-to-all(bf16[32,8,2176]{2,1,0:T(8,128)(2,1)S(1)} %fusion.6), channel_id=1, replica_groups=mesh['frames_0'=4,'frames_1'=4,'frames_2'=2,'heads'=16] {'frames_0','fra..., dimensions={0} | all-to-all | bytes 2228224 | tf_op jit(solution)/shard_map/all_to_all | solution.py:16
  185.4 0.2 convert_reduce_fusion
  185.5 0.2 fusion.24
  185.7 0.1 fusion.16
  185.8 0.1 broadcast_in_dim.11
  185.9 15.0 %all_to_all.46 = bf16[32,8,1024]{2,1,0:T(8,128)(2,1)S(1)} all-to-all(bf16[32,8,1024]{2,1,0:T(8,128)(2,1)S(1)} %broadcast_in_dim.11), channel_id=1, replica_groups=mesh['frames_0'=4,'frames_1'=4,'frames_2'=2,'heads'=16] {'frames_0','fra..., dimensions={0} | all-to-all | bytes 1048576 | tf_op jit(solution)/shard_map/all_to_all | solution.py:16
  200.9 0.3 convolution_convert_fusion.4
  201.2 17.9 %all_to_all.47 = bf16[16,16,256]{2,1,0:T(8,128)(2,1)S(1)} all-to-all(bf16[16,16,256]{2,1,0:T(8,128)(2,1)S(1)} %bitcast.86), channel_id=1, replica_groups=mesh['frames_0'=4,'frames_1'=4,'frames_2'=2,'heads'=16] {'heads'}, dimensions={0} | all-to-all | bytes 262144 | tf_op jit(solution)/shard_map/all_to_all | solution.py:16
  219.1 0.6 add_convert_fusion
  (33 shorter events, 0.4 us)
Async XLA Ops:
  6.5 80.2 %copy-start = (bf16[1152,256]{1,0:T(8,128)(2,1)S(1)}, bf16[1152,256]{1,0:T(8,128)(2,1)}, u32[]{:S(2)}) copy-start(bf16[1152,256]{1,0:T(8,128)(2,1)} %param.13) | copy-start | bytes 1769476
  6.5 80.2 %all-gather.2.cloned.1.call-start = ((), (), s32[]{:S(2)}) async-start(), calls=%async_computation.8 | async-start | bytes 2506752 | tf_op jit(solution)/shard_map/all_gather | solution.py:71
  89.3 1.7 copy-start.6
  89.3 1.8 copy-start.7
  91.9 28.8 %copy-start.4 = (bf16[256,256]{1,0:T(8,128)(2,1)S(1)}, bf16[256,256]{1,0:T(8,128)(2,1)}, u32[]{:S(2)}) copy-start(bf16[256,256]{1,0:T(8,128)(2,1)} %param.15) | copy-start | bytes 393220
  92.5 70.1 %copy-start.5 = (f32[256]{0:T(256)S(1)}, f32[256]{0:T(256)}, u32[]{:S(2)}) copy-start(f32[256]{0:T(256)} %param.16) | copy-start | bytes 3076
  92.5 70.2 %copy-start.1 = (bf16[256,1024]{1,0:T(8,128)(2,1)S(1)}, bf16[256,1024]{1,0:T(8,128)(2,1)}, u32[]{:S(2)}) copy-start(bf16[256,1024]{1,0:T(8,128)(2,1)} %param.18) | copy-start | bytes 1572868
  93.1 69.9 %copy-start.2 = (bf16[256,1024]{1,0:T(8,128)(2,1)S(1)}, bf16[256,1024]{1,0:T(8,128)(2,1)}, u32[]{:S(2)}) copy-start(bf16[256,1024]{1,0:T(8,128)(2,1)} %param.17) | copy-start | bytes 1572868
  163.4 37.5 %copy-start.3 = (bf16[1024,256]{1,0:T(8,128)(2,1)S(1)}, bf16[1024,256]{1,0:T(8,128)(2,1)}, u32[]{:S(2)}) copy-start(bf16[1024,256]{1,0:T(8,128)(2,1)} %param.19) | copy-start | bytes 1572868
Sparse Core Ops, SparseCore 0:
  9.4 77.2 all-gather.1
where the time goes:
time: 227 us
  blocking collectives  138 us (61%)
  waiting for transfers between devices  63.9 us (28%)
  between operations  13.7 us (6%)
  matrix products  6.78 us (3%)
  other arithmetic  2.38 us (1%)
    all_to_all x8, blocking collectives, exchange(): return lax.all_to_all(blocks, axis, split_axis=0, concat_axis=0, tiled=True)  138 us
    all_gather x1, waiting for transfers between devices, on_device(): piece = lax.all_gather(frames, 'heads', axis=1, tiled=True)  63.2 us
  transfers between devices with their start and end apart: 1, of which 1 were waited for; matrix products, arithmetic and copies ran while one was open for 1% of the time, Pallas kernels for 0%

commit v1 on v0

--- a/solution.py
+++ b/solution.py
@@ -68,7 +68,9 @@
     local_query = jnp.dot(latents, w_query, preferred_element_type=F32).astype(BF16)
     queries = collect_rows(local_query, FRAMES)
     width = w_key.shape[1]
-    piece = lax.all_gather(frames, "heads", axis=1, tiled=True)
+    piece = jnp.concatenate(
+        lax.all_to_all(jnp.stack([frames] * lax.axis_size("heads")), "heads", 0, 0), axis=1
+    )
     keys = jnp.dot(piece, w_key, preferred_element_type=F32)
     values = jnp.dot(piece, w_value, preferred_element_type=F32)
     heads_here = width // HDIM

time: 227 us -> 268 us (1.18)
  waiting for transfers between devices: 63.9 us -> 104 us
  starting transfers between devices: 0.01 us -> 15.2 us
  between operations: 13.7 us -> 0.3 us
    all_to_all x0 -> x1, waiting for transfers between devices: none -> 104 us  [on_device(): lax.all_to_all(jnp.stack([frames] * lax.axis_size('heads')), 'heads', 0, 0)]
    all_gather x1 -> x0, waiting for transfers between devices: 63.2 us -> none  [on_device(): piece = lax.all_gather(frames, 'heads', axis=1, tiled=True)]
    all_to_all x0 -> x1, starting transfers between devices: none -> 15.2 us  [on_device(): lax.all_to_all(jnp.stack([frames] * lax.axis_size('heads')), 'heads', 0, 0)]
  transfers between devices with their start and end apart: 1 -> 1, of which waited for: 1 -> 1; matrix products, arithmetic and copies ran while one was open for 1% -> 0% of each run, Pallas kernels for 0% -> 0%
where the time goes in v1:
time: 268 us; the launch traced here: 267 us
  blocking collectives  136 us (51%)
  waiting for transfers between devices  104 us (39%)
  starting transfers between devices  15.2 us (6%)
  matrix products  5.18 us (2%)
  local copies, waits for them, and re-layouts  4.01 us (1%)
    all_to_all x8, blocking collectives, exchange(): return lax.all_to_all(blocks, axis, split_axis=0, concat_axis=0, tiled=True)  136 us
    all_to_all x1, waiting for transfers between devices, on_device(): lax.all_to_all(jnp.stack([frames] * lax.axis_size('heads')), 'heads', 0, 0)  104 us
    all_to_all x1, starting transfers between devices, on_device(): lax.all_to_all(jnp.stack([frames] * lax.axis_size('heads')), 'heads', 0, 0)  15.2 us
  transfers between devices with their start and end apart: 1, of which 1 were waited for; matrix products, arithmetic and copies ran while one was open for 0% of the time, Pallas kernels for 0%

profile of v1, /device:TPU:32, one launch (start us, length us, event | category | flops | bytes accessed | tf_op | source)
XLA Modules:
  0.0 267.1 jit_solution(16939593787214337827)
XLA Ops:
  0.0 1.3 convolution_convert_fusion.7
  1.4 14.9 %all_to_all.45 = bf16[32,8,256]{2,1,0:T(8,128)(2,1)S(1)} all-to-all(bf16[32,8,256]{2,1,0:T(8,128)(2,1)S(1)} %broadcast_in_dim.8), channel_id=1, replica_groups=mesh['frames_0'=4,'frames_1'=4,'frames_2'=2,'heads'=16] {'frames_0','fra..., dimensions={0} | all-to-all | bytes 262144 | tf_op jit(solution)/shard_map/all_to_all | solution.py:16
  16.3 2.6 stack.6
  18.9 15.2 %all-to-all-start = ((bf16[16,1024,72]{1,2,0:T(8,128)(2,1)}), bf16[16,1024,72]{1,2,0:T(8,128)(2,1)S(1)}, u32[]{:S(2)}, u32[]{:S(2)}) async-start(bf16[16,1024,72]{1,2,0:T(8,128)(2,1)} %stack.6), calls=%async_computation | async-start | bytes 4718592 | tf_op jit(solution)/shard_map/all_to_all | solution.py:72
  34.1 104.4 %all-to-all-done = bf16[16,1024,72]{1,2,0:T(8,128)(2,1)S(1)} async-done(((bf16[16,1024,72]{1,2,0:T(8,128)(2,1)}), bf16[16,1024,72]{1,2,0:T(8,128)(2,1)S(1)}, u32[]{:S(2)}, u32[]{:S(2)}) %all-to-all-start) | async-done | bytes 2359328 | tf_op jit(solution)/shard_map/all_to_all | solution.py:72
  138.5 0.9 convolution_convert_fusion.2
  139.4 0.2 copy-done.6
  139.6 0.9 convolution_convert_fusion.3
  140.5 0.5 bitcast_reduce_fusion
  141.0 0.4 fusion.2
  141.4 0.0 copy-start.4
  141.4 0.5 fusion.4
  141.9 0.0 copy-start.5
  141.9 0.0 copy-start.1
  141.9 0.1 copy.83
  142.1 0.2 copy.84
  142.3 0.2 reshape.194
  142.5 0.0 copy-start.2
  142.6 11.6 %all_to_all.46 = bf16[32,17,128]{2,1,0:T(8,128)(2,1)S(1)} all-to-all(bf16[32,17,128]{2,1,0:T(8,128)(2,1)S(1)} %pad_maximum_fusion), channel_id=1, replica_groups=mesh['frames_0'=4,'frames_1'=4,'frames_2'=2,'heads'=16] {'frames_0','fra..., dimensions={0} | all-to-all | bytes 278528 | tf_op jit(solution)/shard_map/all_to_all | solution.py:16
  154.2 0.1 copy.86
  154.4 0.1 fusion.32
  154.5 0.1 subtract_exponential_fusion
  154.6 0.2 fusion.20
  154.8 0.1 copy.92
  154.9 0.1 copy.87
  154.9 0.1 multiply_reduce_fusion.1
  155.1 0.1 fusion.19
  155.2 11.4 %all_to_all.47 = bf16[32,8,256]{2,1,0:T(8,128)(2,1)S(1)} all-to-all(bf16[32,8,256]{2,1,0:T(8,128)(2,1)S(1)} %broadcast_in_dim.9), channel_id=1, replica_groups=mesh['frames_0'=4,'frames_1'=4,'frames_2'=2,'heads'=16] {'frames_0','fra..., dimensions={0} | all-to-all | bytes 262144 | tf_op jit(solution)/shard_map/all_to_all | solution.py:16
  166.6 0.2 convolution_convert_fusion.5
  166.8 23.6 %all_to_all.48 = bf16[16,16,256]{2,1,0:T(8,128)(2,1)S(1)} all-to-all(bf16[16,16,256]{2,1,0:T(8,128)(2,1)S(1)} %bitcast.90), channel_id=1, replica_groups=mesh['frames_0'=4,'frames_1'=4,'frames_2'=2,'heads'=16] {'heads'}, dimensions={0} | all-to-all | bytes 262144 | tf_op jit(solution)/shard_map/all_to_all | solution.py:16
  190.5 19.1 %all_to_all.49 = bf16[16,16,256]{2,1,0:T(8,128)(2,1)S(1)} all-to-all(bf16[16,16,256]{2,1,0:T(8,128)(2,1)S(1)} %broadcast_in_dim.10), channel_id=1, replica_groups=mesh['frames_0'=4,'frames_1'=4,'frames_2'=2,'heads'=16] {'heads'}, dimensions={0} | all-to-all | bytes 262144 | tf_op jit(solution)/shard_map/all_to_all | solution.py:16
  209.6 0.1 multiply_reduce_fusion
  209.7 0.1 reduce_sum.79
  209.8 0.1 copy.93
  210.0 0.3 convolution_convert_fusion
  210.3 0.0 copy-done.2
  210.3 0.3 convolution_convert_fusion.1
  210.7 0.1 fusion.6
  210.7 0.0 copy-start.3
  210.8 22.0 %all_to_all.50 = bf16[32,8,2176]{2,1,0:T(8,128)(2,1)S(1)} all-to-all(bf16[32,8,2176]{2,1,0:T(8,128)(2,1)S(1)} %fusion.6), channel_id=1, replica_groups=mesh['frames_0'=4,'frames_1'=4,'frames_2'=2,'heads'=16] {'frames_0','fra..., dimensions={0} | all-to-all | bytes 2228224 | tf_op jit(solution)/shard_map/all_to_all | solution.py:16
  232.7 0.2 convert_reduce_fusion
  232.9 0.2 fusion.24
  233.1 0.1 fusion.16
  233.2 0.1 broadcast_in_dim.11
  233.3 15.0 %all_to_all.51 = bf16[32,8,1024]{2,1,0:T(8,128)(2,1)S(1)} all-to-all(bf16[32,8,1024]{2,1,0:T(8,128)(2,1)S(1)} %broadcast_in_dim.11), channel_id=1, replica_groups=mesh['frames_0'=4,'frames_1'=4,'frames_2'=2,'heads'=16] {'frames_0','fra..., dimensions={0} | all-to-all | bytes 1048576 | tf_op jit(solution)/shard_map/all_to_all | solution.py:16
  248.2 0.3 convolution_convert_fusion.4
  248.6 17.9 %all_to_all.52 = bf16[16,16,256]{2,1,0:T(8,128)(2,1)S(1)} all-to-all(bf16[16,16,256]{2,1,0:T(8,128)(2,1)S(1)} %bitcast.91), channel_id=1, replica_groups=mesh['frames_0'=4,'frames_1'=4,'frames_2'=2,'heads'=16] {'heads'}, dimensions={0} | all-to-all | bytes 262144 | tf_op jit(solution)/shard_map/all_to_all | solution.py:16
  266.5 0.6 add_convert_fusion
  (31 shorter events, 0.4 us)
Async XLA Ops:
  0.0 138.5 %copy-start = (bf16[1152,256]{1,0:T(8,128)(2,1)S(1)}, bf16[1152,256]{1,0:T(8,128)(2,1)}, u32[]{:S(2)}) copy-start(bf16[1152,256]{1,0:T(8,128)(2,1)} %param.13) | copy-start | bytes 1769476
  18.9 119.7 %all-to-all-start = ((bf16[16,1024,72]{1,2,0:T(8,128)(2,1)}), bf16[16,1024,72]{1,2,0:T(8,128)(2,1)S(1)}, u32[]{:S(2)}, u32[]{:S(2)}) async-start(bf16[16,1024,72]{1,2,0:T(8,128)(2,1)} %stack.6), calls=%async_computation | async-start | bytes 4718592 | tf_op jit(solution)/shard_map/all_to_all | solution.py:72
  138.5 1.1 copy-start.6
  141.4 25.3 %copy-start.4 = (bf16[256,256]{1,0:T(8,128)(2,1)S(1)}, bf16[256,256]{1,0:T(8,128)(2,1)}, u32[]{:S(2)}) copy-start(bf16[256,256]{1,0:T(8,128)(2,1)} %param.15) | copy-start | bytes 393220
  141.9 68.1 %copy-start.5 = (f32[256]{0:T(256)S(1)}, f32[256]{0:T(256)}, u32[]{:S(2)}) copy-start(f32[256]{0:T(256)} %param.16) | copy-start | bytes 3076
  141.9 68.1 %copy-start.1 = (bf16[256,1024]{1,0:T(8,128)(2,1)S(1)}, bf16[256,1024]{1,0:T(8,128)(2,1)}, u32[]{:S(2)}) copy-start(bf16[256,1024]{1,0:T(8,128)(2,1)} %param.18) | copy-start | bytes 1572868
  142.5 67.8 %copy-start.2 = (bf16[256,1024]{1,0:T(8,128)(2,1)S(1)}, bf16[256,1024]{1,0:T(8,128)(2,1)}, u32[]{:S(2)}) copy-start(bf16[256,1024]{1,0:T(8,128)(2,1)} %param.17) | copy-start | bytes 1572868
  210.7 37.5 %copy-start.3 = (bf16[1024,256]{1,0:T(8,128)(2,1)S(1)}, bf16[1024,256]{1,0:T(8,128)(2,1)}, u32[]{:S(2)}) copy-start(bf16[1024,256]{1,0:T(8,128)(2,1)} %param.19) | copy-start | bytes 1572868
